TPU v7x, 32 devices: a whole 2x2x4 slice. The times are simulated.
32 devices in a mesh: rep: 4 (over x, core), grp: 8 (over z, y).
Axes of the slice: x: 2, y: 2, z: 4, core: 2. Of those that a mesh axis runs over, the one named last changes fastest.
Arguments:
- tokens: bfloat16 [8192, 2304], P(('rep', 'grp')), may hold values from -6 to 6
- norm_gain: float32 [2304], replicated, may hold values from 0.25 to 1.75
- key_weight: bfloat16 [2304, 1024], P('grp'), may hold values from -0.125 to 0.125
- key_grad: bfloat16 [8192, 1024], P(('rep', 'grp')), may hold values from -6 to 6
Outputs:
- token_grad: bfloat16 [8192, 2304], P(('rep', 'grp'))
- weight_grad: float32 [2304, 1024], P('grp', 'rep')
- gain_grad: float32 [2304], replicated
All inputs are finite; a program needn't handle non-finite values.
Results may differ from a plain program's by a relative error of at most 0.023.
Values may be sent and summed in bfloat16 or wider, within the bound.
No kernel may reach another device: no remote copies, remote signals or barrier semaphores. Data moves between devices by JAX's collectives and lax.ppermute only.
A program may use at most 64 MiB of HBM per device.

v0:
```python
import jax
import jax.numpy as jnp
from jax import lax
from jax.sharding import PartitionSpec as P


epsilon = 1e-06


def swap(value, axis, flip):
    size = lax.axis_size(axis)
    return lax.ppermute(value, axis, [(i, i ^ flip) for i in range(size)])


def tree_sum(parts):
    while len(parts) > 1:
        parts = [parts[i] + parts[i + 1] for i in range(0, len(parts), 2)]
    return parts[0]


def sum_everywhere(value, axis):
    size = lax.axis_size(axis)
    step = 1
    while step < size:
        radix = min(8, size // step)
        value = tree_sum([value] + [swap(value, axis, step * k) for k in range(1, radix)])
        step *= radix
    return value


def shards(tokens, norm_gain, key_weight, key_grad):
    f32, bf16 = jnp.float32, jnp.bfloat16
    n_rep, n_grp = lax.axis_size("rep"), lax.axis_size("grp")
    rep, grp = lax.axis_index("rep"), lax.axis_index("grp")
    grad_scale = (tokens.shape[0] * n_rep * n_grp) ** (-0.5)
    features, keys = key_weight.shape[0] * n_grp, key_weight.shape[1]
    rows, cols, half = key_weight.shape[0], keys // n_rep, keys // 2
    core = rep % 2

    own = lax.dynamic_slice_in_dim(key_weight, core * half, half, 1)
    pieces = {0: own}
    for flip in range(2, n_grp, 2):
        pieces[flip] = swap(own, "grp", flip)
    for flip in range(0, n_grp, 2):
        pieces[flip + 1] = swap(pieces[flip], "grp", 1)

    wide_tokens = tokens.astype(f32)
    inv_rms = lax.rsqrt(jnp.mean(wide_tokens * wide_tokens, axis=1, keepdims=True) + epsilon)
    normed = (wide_tokens * inv_rms * norm_gain).astype(bf16)

    def partial(flip):
        block = lax.dynamic_slice_in_dim(key_grad, (rep ^ flip) * cols, cols, 1)
        return lax.dot_general(normed, block, (((0,), (0,)), ((), ())), preferred_element_type=f32)

    crossing = {}
    for flip in list(range(2, n_rep, 2)) + [0]:
        crossing[flip] = swap(partial(flip + 1).astype(bf16), "rep", 1)
    sent = {}
    for flip in range(2, n_rep, 2):
        sent[flip] = swap((partial(flip) + crossing[flip].astype(f32)).astype(bf16), "rep", flip)
    section = partial(0) + crossing[0].astype(f32)
    for flip in sent:
        section = section + sent[flip].astype(f32)
    narrow = section.astype(bf16)
    weight_sum = lax.dynamic_slice_in_dim(section, grp * rows, rows, 0)
    arriving = []
    for flip in range(1, n_grp):
        block = lax.dynamic_slice_in_dim(narrow, (grp ^ flip) * rows, rows, 0)
        arriving.append(swap(block, "grp", flip))

    gathered = jnp.zeros((features, half), bf16)
    for flip in range(n_grp):
        gathered = lax.dynamic_update_slice_in_dim(gathered, pieces[flip], (grp ^ flip) * rows, 0)
    other = swap(gathered, "rep", 1)

    def back(weight, at):
        block = lax.dynamic_slice_in_dim(key_grad, at * half, half, 1)
        return lax.dot_general(block, weight, (((1,), (1,)), ((), ())), preferred_element_type=f32)

    d_normed = back(gathered, core) + back(other, 1 - core)
    gain_local = jnp.sum(d_normed * wide_tokens * inv_rms, axis=0)
    gain_total = sum_everywhere(sum_everywhere(gain_local, "rep"), "grp")
    scaled = d_normed * norm_gain
    inner_mean = jnp.mean(scaled * wide_tokens, axis=1, keepdims=True)
    token_grad = (inv_rms * (scaled - wide_tokens * inv_rms * inv_rms * inner_mean)).astype(bf16)
    arriving, token_grad, gain_total = lax.optimization_barrier((arriving, token_grad, gain_total))
    for block in arriving:
        weight_sum = weight_sum + block.astype(f32)
    return (token_grad, weight_sum * grad_scale, gain_total * grad_scale)


def solution(mesh):
    in_specs = (P(("rep", "grp"), None), P(), P("grp", None), P(("rep", "grp"), None))
    out_specs = (P(("rep", "grp"), None), P("grp", "rep"), P())
    return jax.shard_map(shards, mesh=mesh, in_specs=in_specs, out_specs=out_specs, check_vma=False)
```

profile of v0, /device:TPU:0, one launch (start us, length us, event | category | flops | bytes accessed | tf_op | source)
XLA Modules:
  0.0 129.6 jit_solution(11209380394140271452)
XLA Ops:
  3.2 3.0 %collective-permute-start.11 = (bf16[288,512]{1,0:T(8,128)(2,1)}, bf16[288,512]{1,0:T(8,128)(2,1)S(1)}, u32[]{:S(2)}, u32[]{:S(2)}) collective-permute-start(bf16[288,512]{1,0:T(8,128)(2,1)} %get-tuple-element.24), channel_id=1, source_target_pairs={{0,2},{1,3},{2,0},{3,1},{4,6},{5,7},{6,4},{7,5},{8,10},{9,11},{10,... | collective-permute-start | bytes 884744 | tf_op jit(solution)/shard_map/ppermute | solution.py:12
  6.5 1.6 %convolution_convert_fusion = bf16[2304,256]{1,0:T(8,128)(2,1)} fusion(bf16[256,1024]{1,0:T(8,128)(2,1)S(1)} %copy-done, s32[]{:T(128)S(6)} %select_n.61, bf16[256,2304]{1,0:T(8,128)(2,1)S(1)} %copy-done.1, f32[2304]{0:T(1024)S(1)} %copy-done.3, f32[256]{0:T(256)S(1)} %add_rsqrt_fusion), kind=kOutput, calls=%fused_computation.5 | convolution fusion | flops 304939008 | bytes 2503684 | tf_op jit(solution)/shard_map/dot_general | solution.py:53
  9.7 2.6 %collective-permute-start.13 = (bf16[288,512]{1,0:T(8,128)(2,1)}, bf16[288,512]{1,0:T(8,128)(2,1)}, u32[]{:S(2)}, u32[]{:S(2)}) collective-permute-start(bf16[288,512]{1,0:T(8,128)(2,1)} %get-tuple-element.24), channel_id=1, source_target_pairs={{0,4},{1,5},{2,6},{3,7},{4,0},{5,1},{6,2},{7,3},{8,12},{9,13},{10,... | collective-permute-start | bytes 884744 | tf_op jit(solution)/shard_map/ppermute | solution.py:12
  13.4 4.4 %collective-permute-start.12 = (bf16[288,512]{1,0:T(8,128)(2,1)S(1)}, bf16[288,512]{1,0:T(8,128)(2,1)}, u32[]{:S(2)}, u32[]{:S(2)}) collective-permute-start(bf16[288,512]{1,0:T(8,128)(2,1)S(1)} %collective-permute-done.11), channel_id=1, source_target_pairs={{0,1},{1,0},{2,3},{3,2},{4,5},{5,4},{6,7},{7,6},{8,9},{9,8},{10,11... | collective-permute-start | bytes 884744 | tf_op jit(solution)/shard_map/ppermute | solution.py:12
  17.8 1.7 %convolution_convert_fusion.1 = bf16[2304,256]{1,0:T(8,128)(2,1)} fusion(bf16[256,1024]{1,0:T(8,128)(2,1)S(1)} %copy-done, s32[]{:T(128)S(6)} %select_n.59, bf16[256,2304]{1,0:T(8,128)(2,1)S(1)} %copy-done.1, f32[2304]{0:T(1024)S(1)} %copy-done.3, f32[256]{0:T(256)S(1)} %add_rsqrt_fusion), kind=kOutput, calls=%fused_computation.6 | convolution fusion | flops 304939008 | bytes 2503684 | tf_op jit(solution)/shard_map/dot_general | solution.py:53
  19.5 13.9 %collective-permute-done.13 = bf16[288,512]{1,0:T(8,128)(2,1)} collective-permute-done((bf16[288,512]{1,0:T(8,128)(2,1)}, bf16[288,512]{1,0:T(8,128)(2,1)}, u32[]{:S(2)}, u32[]{:S(2)}) %collective-permute-start.13) | collective-permute-done | bytes 294944 | tf_op jit(solution)/shard_map/ppermute | solution.py:12
  35.5 1.7 %constant_dynamic-update-slice_fusion.6 = bf16[2304,512]{1,0:T(8,128)(2,1)} fusion(bf16[2304,512]{1,0:T(8,128)(2,1)} %get-tuple-element.23, bf16[288,512]{1,0:T(8,128)(2,1)} %collective-permute-done.10, s32[]{:T(128)S(6)} %select_n.62), kind=kLoop, calls=%fused_computation.40 | loop fusion | bytes 589828 | tf_op jit(solution)/shard_map/dynamic_update_slice | solution.py:73
  37.9 1.7 %constant_dynamic-update-slice_fusion.4 = bf16[2304,512]{1,0:T(8,128)(2,1)} fusion(bf16[2304,512]{1,0:T(8,128)(2,1)} %constant_dynamic-update-slice_fusion.5, bf16[288,512]{1,0:T(8,128)(2,1)} %collective-permute-done.12, s32[]{:T(128)S(6)} %select_n.64), kind=kLoop, calls=%fused_computation.38 | loop fusion | bytes 589828 | tf_op jit(solution)/shard_map/dynamic_update_slice | solution.py:73
  39.6 1.7 %constant_dynamic-update-slice_fusion.3 = bf16[2304,512]{1,0:T(8,128)(2,1)} fusion(bf16[2304,512]{1,0:T(8,128)(2,1)} %constant_dynamic-update-slice_fusion.4, bf16[288,512]{1,0:T(8,128)(2,1)} %collective-permute-done.13, s32[]{:T(128)S(6)} %select_n.65), kind=kLoop, calls=%fused_computation.37 | loop fusion | bytes 589828 | tf_op jit(solution)/shard_map/dynamic_update_slice | solution.py:73
  41.3 2.2 %collective-permute-done.14 = bf16[288,512]{1,0:T(8,128)(2,1)S(1)} collective-permute-done((bf16[288,512]{1,0:T(8,128)(2,1)}, bf16[288,512]{1,0:T(8,128)(2,1)S(1)}, u32[]{:S(2)}, u32[]{:S(2)}) %collective-permute-start.14) | collective-permute-done | bytes 294944 | tf_op jit(solution)/shard_map/ppermute | solution.py:12
  45.0 2.6 %collective-permute-done.16 = bf16[288,512]{1,0:T(8,128)(2,1)S(1)} collective-permute-done((bf16[288,512]{1,0:T(8,128)(2,1)S(1)}, bf16[288,512]{1,0:T(8,128)(2,1)S(1)}, u32[]{:S(2)}, u32[]{:S(2)}) %collective-permute-start.16) | collective-permute-done | bytes 294944 | tf_op jit(solution)/shard_map/ppermute | solution.py:12
  48.3 3.0 %add_convert_fusion = bf16[2304,256]{1,0:T(8,128)(2,1)} fusion(bf16[2304,256]{1,0:T(8,128)(2,1)} %collective-permute-done.1, bf16[256,1024]{1,0:T(8,128)(2,1)S(1)} %copy-done, s32[]{:T(128)S(6)} %select_n.60, bf16[256,2304]{1,0:T(8,128)(2,1)S(1)} %copy-done.1, f32[2304]{0:T(1024)S(1)} %copy-done.3, f32[256]{0:T(256)S(1)} %add_rsqrt_fusion), kind=kOutput, calls=%fused_computation.19 | convolution fusion | flops 306118656 | bytes 3683332 | tf_op jit(solution)/shard_map/dot_general | solution.py:53
  53.4 26.6 %collective-permute-done.2 = bf16[2304,256]{1,0:T(8,128)(2,1)} collective-permute-done((bf16[2304,256]{1,0:T(8,128)(2,1)}, bf16[2304,256]{1,0:T(8,128)(2,1)}, u32[]{:S(2)}, u32[]{:S(2)}) %collective-permute-start.2) | collective-permute-done | bytes 1179680 | tf_op jit(solution)/shard_map/ppermute | solution.py:12
  81.6 2.5 %fusion.11 = f32[256,2304]{1,0:T(8,128)S(1)} fusion(bf16[2304,512]{1,0:T(8,128)(2,1)} %collective-permute-done.17, bf16[256,1024]{1,0:T(8,128)(2,1)S(1)} %copy-done, s32[]{:T(128)S(6)} %select_n.72), kind=kOutput, calls=%fused_computation.21 | convolution fusion | flops 603979776 | bytes 4980740 | tf_op jit(solution)/shard_map/dot_general | solution.py:78
  84.1 2.7 %fusion.10 = (f32[2304]{0:T(1024)S(1)}, f32[256]{0:T(256)S(1)}, f32[256,2304]{1,0:T(8,128)S(1)}) fusion(bf16[256,2304]{1,0:T(8,128)(2,1)S(1)} %copy-done.1, f32[256]{0:T(256)S(1)} %add_rsqrt_fusion, f32[2304]{0:T(1024)S(1)} %copy-done.3, f32[256,2304]{1,0:T(8,128)S(1)} %fusion.11, bf16[2304,512]{1,0:T(8,128)(2,1)} %constant_dynamic-update-slice_fusion, ...), kind=kOutput, calls=%fused_computation.17 | convolution fusion | flops 608695808 | bytes 8543236 | tf_op jit(solution)/shard_map/dot_general | solution.py:78
  93.0 2.0 %collective-permute-start.23 = (f32[2304]{0:T(1024)S(1)}, f32[2304]{0:T(1024)S(1)}, u32[]{:S(2)}, u32[]{:S(2)}) collective-permute-start(f32[2304]{0:T(1024)S(1)} %add_add_fusion.1), channel_id=1, source_target_pairs={{0,3},{1,2},{2,1},{3,0},{4,7},{5,6},{6,5},{7,4},{8,11},{9,10},{10,... | collective-permute-start | bytes 27656 | tf_op jit(solution)/shard_map/ppermute | solution.py:12
  96.4 1.6 %collective-permute-start.25 = (f32[2304]{0:T(1024)S(1)}, f32[2304]{0:T(1024)S(1)}, u32[]{:S(2)}, u32[]{:S(2)}) collective-permute-start(f32[2304]{0:T(1024)S(1)} %add_add_fusion.1), channel_id=1, source_target_pairs={{0,5},{1,4},{2,7},{3,6},{4,1},{5,0},{6,3},{7,2},{8,13},{9,12},{10,... | collective-permute-start | bytes 27656 | tf_op jit(solution)/shard_map/ppermute | solution.py:12
  98.0 2.5 %collective-permute-start.26 = (f32[2304]{0:T(1024)S(1)}, f32[2304]{0:T(1024)S(1)}, u32[]{:S(2)}, u32[]{:S(2)}) collective-permute-start(f32[2304]{0:T(1024)S(1)} %add_add_fusion.1), channel_id=1, source_target_pairs={{0,6},{1,7},{2,4},{3,5},{4,2},{5,3},{6,0},{7,1},{8,14},{9,15},{10,... | collective-permute-start | bytes 27656 | tf_op jit(solution)/shard_map/ppermute | solution.py:12
  100.5 2.3 %collective-permute-start.27 = (f32[2304]{0:T(1024)S(1)}, f32[2304]{0:T(1024)S(1)}, u32[]{:S(2)}, u32[]{:S(2)}) collective-permute-start(f32[2304]{0:T(1024)S(1)} %add_add_fusion.1), channel_id=1, source_target_pairs={{0,7},{1,6},{2,5},{3,4},{4,3},{5,2},{6,1},{7,0},{8,15},{9,14},{10,... | collective-permute-start | bytes 27656 | tf_op jit(solution)/shard_map/ppermute | solution.py:12
  102.8 1.7 %fusion.6 = bf16[256,2304]{1,0:T(8,128)(2,1)} fusion(bf16[256,2304]{1,0:T(8,128)(2,1)S(1)} %copy-done.1, f32[256,2304]{1,0:T(8,128)S(1)} %get-tuple-element.34, f32[256]{0:T(256)S(1)} %broadcast_multiply_fusion.1, f32[2304]{0:T(1024)S(1)} %copy-done.3, f32[256]{0:T(256)S(1)} %add_rsqrt_fusion), kind=kLoop, calls=%fused_computation.13 | loop fusion | flops 4718592 | bytes 4729856 | tf_op jit(solution)/shard_map/convert_element_type | solution.py:85
  104.5 3.0 %collective-permute-start.6 = (bf16[288,256]{1,0:T(8,128)(2,1)S(1)}, bf16[288,256]{1,0:T(8,128)(2,1)S(1)}, u32[]{:S(2)}, u32[]{:S(2)}) collective-permute-start(bf16[288,256]{1,0:T(8,128)(2,1)S(1)} %get-tuple-element.30), channel_id=1, source_target_pairs={{0,4},{1,5},{2,6},{3,7},{4,0},{5,1},{6,2},{7,3},{8,12},{9,13},{10,... | collective-permute-start | bytes 442376 | tf_op jit(solution)/shard_map/ppermute | solution.py:12
  109.9 2.4 %collective-permute-start.9 = (bf16[288,256]{1,0:T(8,128)(2,1)S(1)}, bf16[288,256]{1,0:T(8,128)(2,1)S(1)}, u32[]{:S(2)}, u32[]{:S(2)}) collective-permute-start(bf16[288,256]{1,0:T(8,128)(2,1)S(1)} %get-tuple-element.27), channel_id=1, source_target_pairs={{0,7},{1,6},{2,5},{3,4},{4,3},{5,2},{6,1},{7,0},{8,15},{9,14},{10,... | collective-permute-start | bytes 442376 | tf_op jit(solution)/shard_map/ppermute | solution.py:12
  112.4 11.3 %collective-permute-done.6 = bf16[288,256]{1,0:T(8,128)(2,1)S(1)} collective-permute-done((bf16[288,256]{1,0:T(8,128)(2,1)S(1)}, bf16[288,256]{1,0:T(8,128)(2,1)S(1)}, u32[]{:S(2)}, u32[]{:S(2)}) %collective-permute-start.6) | collective-permute-done | bytes 147488 | tf_op jit(solution)/shard_map/ppermute | solution.py:12
  123.6 4.4 %collective-permute-done.7 = bf16[288,256]{1,0:T(8,128)(2,1)S(1)} collective-permute-done((bf16[288,256]{1,0:T(8,128)(2,1)S(1)}, bf16[288,256]{1,0:T(8,128)(2,1)S(1)}, u32[]{:S(2)}, u32[]{:S(2)}) %collective-permute-start.7) | collective-permute-done | bytes 147488 | tf_op jit(solution)/shard_map/ppermute | solution.py:12
  (65 shorter events, 25.6 us)
Async XLA Ops:
  3.2 10.3 %collective-permute-start.11 = (bf16[288,512]{1,0:T(8,128)(2,1)}, bf16[288,512]{1,0:T(8,128)(2,1)S(1)}, u32[]{:S(2)}, u32[]{:S(2)}) collective-permute-start(bf16[288,512]{1,0:T(8,128)(2,1)} %get-tuple-element.24), channel_id=1, source_target_pairs={{0,2},{1,3},{2,0},{3,1},{4,6},{5,7},{6,4},{7,5},{8,10},{9,11},{10,... | collective-permute-start | bytes 884744 | tf_op jit(solution)/shard_map/ppermute | solution.py:12
  8.2 40.1 %collective-permute-start.1 = (bf16[2304,256]{1,0:T(8,128)(2,1)}, bf16[2304,256]{1,0:T(8,128)(2,1)}, u32[]{:S(2)}, u32[]{:S(2)}) collective-permute-start(bf16[2304,256]{1,0:T(8,128)(2,1)} %convolution_convert_fusion), channel_id=1, source_target_pairs={{0,8},{8,0},{16,24},{24,16},{1,9},{9,1},{17,25},{25,17},{2,10},{10... | collective-permute-start | bytes 3538952 | tf_op jit(solution)/shard_map/ppermute | solution.py:12
  8.2 11.3 %collective-permute-start.10 = (bf16[288,512]{1,0:T(8,128)(2,1)}, bf16[288,512]{1,0:T(8,128)(2,1)}, u32[]{:S(2)}, u32[]{:S(2)}) collective-permute-start(bf16[288,512]{1,0:T(8,128)(2,1)} %get-tuple-element.24), channel_id=1, source_target_pairs={{0,1},{1,0},{2,3},{3,2},{4,5},{5,4},{6,7},{7,6},{8,9},{9,8},{10,11... | collective-permute-start | bytes 884744 | tf_op jit(solution)/shard_map/ppermute | solution.py:12
  9.7 23.7 %collective-permute-start.13 = (bf16[288,512]{1,0:T(8,128)(2,1)}, bf16[288,512]{1,0:T(8,128)(2,1)}, u32[]{:S(2)}, u32[]{:S(2)}) collective-permute-start(bf16[288,512]{1,0:T(8,128)(2,1)} %get-tuple-element.24), channel_id=1, source_target_pairs={{0,4},{1,5},{2,6},{3,7},{4,0},{5,1},{6,2},{7,3},{8,12},{9,13},{10,... | collective-permute-start | bytes 884744 | tf_op jit(solution)/shard_map/ppermute | solution.py:12
  12.3 21.7 %collective-permute-start.15 = (bf16[288,512]{1,0:T(8,128)(2,1)}, bf16[288,512]{1,0:T(8,128)(2,1)S(1)}, u32[]{:S(2)}, u32[]{:S(2)}) collective-permute-start(bf16[288,512]{1,0:T(8,128)(2,1)} %get-tuple-element.24), channel_id=1, source_target_pairs={{0,6},{1,7},{2,4},{3,5},{4,2},{5,3},{6,0},{7,1},{8,14},{9,15},{10,... | collective-permute-start | bytes 884744 | tf_op jit(solution)/shard_map/ppermute | solution.py:12
  13.4 24.5 %collective-permute-start.12 = (bf16[288,512]{1,0:T(8,128)(2,1)S(1)}, bf16[288,512]{1,0:T(8,128)(2,1)}, u32[]{:S(2)}, u32[]{:S(2)}) collective-permute-start(bf16[288,512]{1,0:T(8,128)(2,1)S(1)} %collective-permute-done.11), channel_id=1, source_target_pairs={{0,1},{1,0},{2,3},{3,2},{4,5},{5,4},{6,7},{7,6},{8,9},{9,8},{10,11... | collective-permute-start | bytes 884744 | tf_op jit(solution)/shard_map/ppermute | solution.py:12
  19.5 33.9 %collective-permute-start = (bf16[2304,256]{1,0:T(8,128)(2,1)}, bf16[2304,256]{1,0:T(8,128)(2,1)S(1)}, u32[]{:S(2)}, u32[]{:S(2)}) collective-permute-start(bf16[2304,256]{1,0:T(8,128)(2,1)} %convolution_convert_fusion.1), channel_id=1, source_target_pairs={{0,8},{8,0},{16,24},{24,16},{1,9},{9,1},{17,25},{25,17},{2,10},{10... | collective-permute-start | bytes 3538952 | tf_op jit(solution)/shard_map/ppermute | solution.py:12
  33.4 10.1 %collective-permute-start.14 = (bf16[288,512]{1,0:T(8,128)(2,1)}, bf16[288,512]{1,0:T(8,128)(2,1)S(1)}, u32[]{:S(2)}, u32[]{:S(2)}) collective-permute-start(bf16[288,512]{1,0:T(8,128)(2,1)} %collective-permute-done.13), channel_id=1, source_target_pairs={{0,1},{1,0},{2,3},{3,2},{4,5},{5,4},{6,7},{7,6},{8,9},{9,8},{10,11... | collective-permute-start | bytes 884744 | tf_op jit(solution)/shard_map/ppermute | solution.py:12
  34.0 13.6 %collective-permute-start.16 = (bf16[288,512]{1,0:T(8,128)(2,1)S(1)}, bf16[288,512]{1,0:T(8,128)(2,1)S(1)}, u32[]{:S(2)}, u32[]{:S(2)}) collective-permute-start(bf16[288,512]{1,0:T(8,128)(2,1)S(1)} %collective-permute-done.15), channel_id=1, source_target_pairs={{0,1},{1,0},{2,3},{3,2},{4,5},{5,4},{6,7},{7,6},{8,9},{9,8},{10,11... | collective-permute-start | bytes 884744 | tf_op jit(solution)/shard_map/ppermute | solution.py:12
  48.3 33.3 %collective-permute-start.17 = (bf16[2304,512]{1,0:T(8,128)(2,1)}, bf16[2304,512]{1,0:T(8,128)(2,1)}, u32[]{:S(2)}, u32[]{:S(2)}) collective-permute-start(bf16[2304,512]{1,0:T(8,128)(2,1)} %constant_dynamic-update-slice_fusion), channel_id=1, source_target_pairs={{0,8},{8,0},{16,24},{24,16},{1,9},{9,1},{17,25},{25,17},{2,10},{10... | collective-permute-start | bytes 7077896 | tf_op jit(solution)/shard_map/ppermute | solution.py:12
  51.3 28.7 %collective-permute-start.2 = (bf16[2304,256]{1,0:T(8,128)(2,1)}, bf16[2304,256]{1,0:T(8,128)(2,1)}, u32[]{:S(2)}, u32[]{:S(2)}) collective-permute-start(bf16[2304,256]{1,0:T(8,128)(2,1)} %add_convert_fusion), channel_id=1, source_target_pairs={{0,16},{8,24},{16,0},{24,8},{1,17},{9,25},{17,1},{25,9},{2,18},{10... | collective-permute-start | bytes 3538952 | tf_op jit(solution)/shard_map/ppermute | solution.py:12
  89.4 7.0 %collective-permute-start.4 = (bf16[288,256]{1,0:T(8,128)(2,1)S(1)}, bf16[288,256]{1,0:T(8,128)(2,1)S(1)}, u32[]{:S(2)}, u32[]{:S(2)}) collective-permute-start(bf16[288,256]{1,0:T(8,128)(2,1)S(1)} %get-tuple-element.32), channel_id=1, source_target_pairs={{0,2},{1,3},{2,0},{3,1},{4,6},{5,7},{6,4},{7,5},{8,10},{9,11},{10,... | collective-permute-start | bytes 442376 | tf_op jit(solution)/shard_map/ppermute | solution.py:12
  91.6 6.4 %collective-permute-start.21 = (f32[2304]{0:T(1024)S(1)}, f32[2304]{0:T(1024)S(1)}, u32[]{:S(2)}, u32[]{:S(2)}) collective-permute-start(f32[2304]{0:T(1024)S(1)} %add_add_fusion.1), channel_id=1, source_target_pairs={{0,1},{1,0},{2,3},{3,2},{4,5},{5,4},{6,7},{7,6},{8,9},{9,8},{10,11... | collective-permute-start | bytes 27656 | tf_op jit(solution)/shard_map/ppermute | solution.py:12
  92.1 8.4 %collective-permute-start.22 = (f32[2304]{0:T(1024)S(1)}, f32[2304]{0:T(1024)S(1)}, u32[]{:S(2)}, u32[]{:S(2)}) collective-permute-start(f32[2304]{0:T(1024)S(1)} %add_add_fusion.1), channel_id=1, source_target_pairs={{0,2},{1,3},{2,0},{3,1},{4,6},{5,7},{6,4},{7,5},{8,10},{9,11},{10,... | collective-permute-start | bytes 27656 | tf_op jit(solution)/shard_map/ppermute | solution.py:12
  93.0 11.5 %collective-permute-start.23 = (f32[2304]{0:T(1024)S(1)}, f32[2304]{0:T(1024)S(1)}, u32[]{:S(2)}, u32[]{:S(2)}) collective-permute-start(f32[2304]{0:T(1024)S(1)} %add_add_fusion.1), channel_id=1, source_target_pairs={{0,3},{1,2},{2,1},{3,0},{4,7},{5,6},{6,5},{7,4},{8,11},{9,10},{10,... | collective-permute-start | bytes 27656 | tf_op jit(solution)/shard_map/ppermute | solution.py:12
  95.1 9.4 %collective-permute-start.24 = (f32[2304]{0:T(1024)S(1)}, f32[2304]{0:T(1024)S(1)}, u32[]{:S(2)}, u32[]{:S(2)}) collective-permute-start(f32[2304]{0:T(1024)S(1)} %add_add_fusion.1), channel_id=1, source_target_pairs={{0,4},{1,5},{2,6},{3,7},{4,0},{5,1},{6,2},{7,3},{8,12},{9,13},{10,... | collective-permute-start | bytes 27656 | tf_op jit(solution)/shard_map/ppermute | solution.py:12
  96.4 11.1 %collective-permute-start.25 = (f32[2304]{0:T(1024)S(1)}, f32[2304]{0:T(1024)S(1)}, u32[]{:S(2)}, u32[]{:S(2)}) collective-permute-start(f32[2304]{0:T(1024)S(1)} %add_add_fusion.1), channel_id=1, source_target_pairs={{0,5},{1,4},{2,7},{3,6},{4,1},{5,0},{6,3},{7,2},{8,13},{9,12},{10,... | collective-permute-start | bytes 27656 | tf_op jit(solution)/shard_map/ppermute | solution.py:12
  98.0 10.5 %collective-permute-start.26 = (f32[2304]{0:T(1024)S(1)}, f32[2304]{0:T(1024)S(1)}, u32[]{:S(2)}, u32[]{:S(2)}) collective-permute-start(f32[2304]{0:T(1024)S(1)} %add_add_fusion.1), channel_id=1, source_target_pairs={{0,6},{1,7},{2,4},{3,5},{4,2},{5,3},{6,0},{7,1},{8,14},{9,15},{10,... | collective-permute-start | bytes 27656 | tf_op jit(solution)/shard_map/ppermute | solution.py:12
  100.5 9.4 %collective-permute-start.27 = (f32[2304]{0:T(1024)S(1)}, f32[2304]{0:T(1024)S(1)}, u32[]{:S(2)}, u32[]{:S(2)}) collective-permute-start(f32[2304]{0:T(1024)S(1)} %add_add_fusion.1), channel_id=1, source_target_pairs={{0,7},{1,6},{2,5},{3,4},{4,3},{5,2},{6,1},{7,0},{8,15},{9,14},{10,... | collective-permute-start | bytes 27656 | tf_op jit(solution)/shard_map/ppermute | solution.py:12
  104.5 7.8 %collective-permute-start.5 = (bf16[288,256]{1,0:T(8,128)(2,1)S(1)}, bf16[288,256]{1,0:T(8,128)(2,1)S(1)}, u32[]{:S(2)}, u32[]{:S(2)}) collective-permute-start(bf16[288,256]{1,0:T(8,128)(2,1)S(1)} %get-tuple-element.31), channel_id=1, source_target_pairs={{0,3},{1,2},{2,1},{3,0},{4,7},{5,6},{6,5},{7,4},{8,11},{9,10},{10,... | collective-permute-start | bytes 442376 | tf_op jit(solution)/shard_map/ppermute | solution.py:12
  104.5 19.1 %collective-permute-start.6 = (bf16[288,256]{1,0:T(8,128)(2,1)S(1)}, bf16[288,256]{1,0:T(8,128)(2,1)S(1)}, u32[]{:S(2)}, u32[]{:S(2)}) collective-permute-start(bf16[288,256]{1,0:T(8,128)(2,1)S(1)} %get-tuple-element.30), channel_id=1, source_target_pairs={{0,4},{1,5},{2,6},{3,7},{4,0},{5,1},{6,2},{7,3},{8,12},{9,13},{10,... | collective-permute-start | bytes 442376 | tf_op jit(solution)/shard_map/ppermute | solution.py:12
  107.5 20.6 %collective-permute-start.7 = (bf16[288,256]{1,0:T(8,128)(2,1)S(1)}, bf16[288,256]{1,0:T(8,128)(2,1)S(1)}, u32[]{:S(2)}, u32[]{:S(2)}) collective-permute-start(bf16[288,256]{1,0:T(8,128)(2,1)S(1)} %get-tuple-element.29), channel_id=1, source_target_pairs={{0,5},{1,4},{2,7},{3,6},{4,1},{5,0},{6,3},{7,2},{8,13},{9,12},{10,... | collective-permute-start | bytes 442376 | tf_op jit(solution)/shard_map/ppermute | solution.py:12
  108.5 19.6 %collective-permute-start.8 = (bf16[288,256]{1,0:T(8,128)(2,1)S(1)}, bf16[288,256]{1,0:T(8,128)(2,1)S(1)}, u32[]{:S(2)}, u32[]{:S(2)}) collective-permute-start(bf16[288,256]{1,0:T(8,128)(2,1)S(1)} %get-tuple-element.28), channel_id=1, source_target_pairs={{0,6},{1,7},{2,4},{3,5},{4,2},{5,3},{6,0},{7,1},{8,14},{9,15},{10,... | collective-permute-start | bytes 442376 | tf_op jit(solution)/shard_map/ppermute | solution.py:12
  109.9 18.2 %collective-permute-start.9 = (bf16[288,256]{1,0:T(8,128)(2,1)S(1)}, bf16[288,256]{1,0:T(8,128)(2,1)S(1)}, u32[]{:S(2)}, u32[]{:S(2)}) collective-permute-start(bf16[288,256]{1,0:T(8,128)(2,1)S(1)} %get-tuple-element.27), channel_id=1, source_target_pairs={{0,7},{1,6},{2,5},{3,4},{4,3},{5,2},{6,1},{7,0},{8,15},{9,14},{10,... | collective-permute-start | bytes 442376 | tf_op jit(solution)/shard_map/ppermute | solution.py:12
  (8 other events, 35.5 us)
where the time goes:
time: 132 us; the launch traced here: 130 us
  waiting for transfers between devices  63.4 us (48%)
  starting transfers between devices  37.6 us (28%)
  matrix products  12.1 us (9%)
  local copies, waits for them, and re-layouts  10.6 us (8%)
  other arithmetic  5.14 us (4%)
    ppermute x28, waiting for transfers between devices, swap(): return lax.ppermute(value, axis, [(i, i ^ flip) for i in range(size)])  63.4 us
    ppermute x28, starting transfers between devices, swap(): return lax.ppermute(value, axis, [(i, i ^ flip) for i in range(size)])  37.6 us
    dynamic_update_slice x8, local copies, waits for them, and re-layouts, shards(): lax.dynamic_update_slice_in_dim(gathered, pieces[flip], (grp ^ flip) * ro...  8.91 us
    dot_general x4, matrix products, partial(): lax.dot_general(normed, block, (((0,), (0,)), ((), ())), preferred_elemen...  6.9 us
    dot_general x2, matrix products, back(): lax.dot_general(block, weight, (((1,), (1,)), ((), ())), preferred_elemen...  5.19 us
  transfers between devices with their start and end apart: 28, of which 9 were waited for; matrix products, arithmetic and copies ran while one was open for 14% of the time, Pallas kernels for 0%

commit v1 on v0

--- a/solution.py
+++ b/solution.py
@@ -33,15 +33,18 @@
     n_rep, n_grp = lax.axis_size("rep"), lax.axis_size("grp")
     rep, grp = lax.axis_index("rep"), lax.axis_index("grp")
     grad_scale = (tokens.shape[0] * n_rep * n_grp) ** (-0.5)
-    features, keys = key_weight.shape[0] * n_grp, key_weight.shape[1]
-    rows, cols, half = key_weight.shape[0], keys // n_rep, keys // 2
+    rows, keys = key_weight.shape
+    cols, half = keys // n_rep, keys // 2
     core = rep % 2
 
     own = lax.dynamic_slice_in_dim(key_weight, core * half, half, 1)
-    pieces = {0: own}
+    pieces = {0: own, 1: swap(own, "grp", 1)}
     for flip in range(2, n_grp, 2):
-        pieces[flip] = swap(own, "grp", flip)
-    for flip in range(0, n_grp, 2):
+        if flip == 2 or flip % 4 == 0:
+            pieces[flip] = swap(own, "grp", flip)
+    for flip in range(6, n_grp, 4):
+        pieces[flip] = swap(pieces[flip - 2], "grp", 2)
+    for flip in range(2, n_grp, 2):
         pieces[flip + 1] = swap(pieces[flip], "grp", 1)
 
     wide_tokens = tokens.astype(f32)
@@ -68,8 +71,9 @@
         block = lax.dynamic_slice_in_dim(narrow, (grp ^ flip) * rows, rows, 0)
         arriving.append(swap(block, "grp", flip))
 
-    gathered = jnp.zeros((features, half), bf16)
-    for flip in range(n_grp):
+    canvas, pieces[1] = lax.optimization_barrier((own, pieces[1]))
+    gathered = jnp.tile(canvas, (n_grp, 1))
+    for flip in range(1, n_grp):
         gathered = lax.dynamic_update_slice_in_dim(gathered, pieces[flip], (grp ^ flip) * rows, 0)
     other = swap(gathered, "rep", 1)
 

time: 132 us -> 125 us (0.947)
  the two profiles are of different devices: /device:TPU:0 before, /device:TPU:8 now
where the time goes in v1:
time: 125 us
  waiting for transfers between devices  54.9 us (44%)
  starting transfers between devices  35.4 us (28%)
  matrix products  14.3 us (11%)
  local copies, waits for them, and re-layouts  12.8 us (10%)
  other arithmetic  6.41 us (5%)
    ppermute x28, waiting for transfers between devices, swap(): return lax.ppermute(value, axis, [(i, i ^ flip) for i in range(size)])  54.9 us
    ppermute x28, starting transfers between devices, swap(): return lax.ppermute(value, axis, [(i, i ^ flip) for i in range(size)])  35.4 us
    dynamic_update_slice x7, local copies, waits for them, and re-layouts, shards(): lax.dynamic_update_slice_in_dim(gathered, pieces[flip], (grp ^ flip) * ro...  10 us
    dot_general x4, matrix products, partial(): lax.dot_general(normed, block, (((0,), (0,)), ((), ())), preferred_elemen...  9.09 us
    dot_general x2, matrix products, back(): lax.dot_general(block, weight, (((1,), (1,)), ((), ())), preferred_elemen...  5.19 us
  transfers between devices with their start and end apart: 28, of which 8 were waited for; matrix products, arithmetic and copies ran while one was open for 21% of the time, Pallas kernels for 0%

profile of v1, /device:TPU:8, one launch (start us, length us, event | category | flops | bytes accessed | tf_op | source)
XLA Modules:
  0.0 124.6 jit_solution(16851236148283997944)
XLA Ops:
  1.8 3.0 %collective-permute-start.13 = (bf16[288,512]{1,0:T(8,128)(2,1)S(1)}, bf16[288,512]{1,0:T(8,128)(2,1)}, u32[]{:S(2)}, u32[]{:S(2)}) collective-permute-start(bf16[288,512]{1,0:T(8,128)(2,1)S(1)} %constant_dynamic-slice_fusion), channel_id=1, source_target_pairs={{0,4},{1,5},{2,6},{3,7},{4,0},{5,1},{6,2},{7,3},{8,12},{9,13},{10,... | collective-permute-start | bytes 884744 | tf_op jit(solution)/shard_map/ppermute | solution.py:12
  6.4 2.9 %convolution_convert_fusion = bf16[2304,256]{1,0:T(8,128)(2,1)} fusion(bf16[256,1024]{1,0:T(8,128)(2,1)} %param.7, s32[]{:T(128)S(6)} %select_n.60, bf16[256,2304]{1,0:T(8,128)(2,1)} %param.4, f32[2304]{0:T(1024)} %param.5, f32[256]{0:T(256)S(1)} %add_rsqrt_fusion), kind=kOutput, calls=%fused_computation.5 | convolution fusion | flops 304939008 | bytes 2503684 | tf_op jit(solution)/shard_map/dot_general | solution.py:56
  10.9 3.7 %collective-permute-done.11 = bf16[288,512]{1,0:T(8,128)(2,1)} collective-permute-done((bf16[288,512]{1,0:T(8,128)(2,1)S(1)}, bf16[288,512]{1,0:T(8,128)(2,1)}, u32[]{:S(2)}, u32[]{:S(2)}) %collective-permute-start.11) | collective-permute-done | bytes 294944 | tf_op jit(solution)/shard_map/ppermute | solution.py:12
  16.3 1.8 %collective-permute-done.13 = bf16[288,512]{1,0:T(8,128)(2,1)} collective-permute-done((bf16[288,512]{1,0:T(8,128)(2,1)S(1)}, bf16[288,512]{1,0:T(8,128)(2,1)}, u32[]{:S(2)}, u32[]{:S(2)}) %collective-permute-start.13) | collective-permute-done | bytes 294944 | tf_op jit(solution)/shard_map/ppermute | solution.py:12
  19.7 2.6 %convolution_convert_fusion.1 = bf16[2304,256]{1,0:T(8,128)(2,1)} fusion(bf16[256,1024]{1,0:T(8,128)(2,1)} %param.7, s32[]{:T(128)S(6)} %select_n.58, bf16[256,2304]{1,0:T(8,128)(2,1)S(1)} %copy-done.1, f32[2304]{0:T(1024)S(1)} %copy-done.4, f32[256]{0:T(256)S(1)} %add_rsqrt_fusion), kind=kOutput, calls=%fused_computation.6 | convolution fusion | flops 304939008 | bytes 2500612 | tf_op jit(solution)/shard_map/dot_general | solution.py:56
  25.5 1.7 %constant_dynamic-update-slice_fusion.6 = bf16[2304,512]{1,0:T(8,128)(2,1)} fusion(bf16[2304,512]{1,0:T(8,128)(2,1)} %bitcast, bf16[288,512]{1,0:T(8,128)(2,1)} %copy-done.3, s32[]{:T(128)S(6)} %select_n.61), kind=kLoop, calls=%fused_computation.40 | loop fusion | bytes 589828 | tf_op jit(solution)/shard_map/dynamic_update_slice | solution.py:77
  27.2 1.7 %constant_dynamic-update-slice_fusion.5 = bf16[2304,512]{1,0:T(8,128)(2,1)} fusion(bf16[2304,512]{1,0:T(8,128)(2,1)} %constant_dynamic-update-slice_fusion.6, bf16[288,512]{1,0:T(8,128)(2,1)} %collective-permute-done.11, s32[]{:T(128)S(6)} %select_n.62), kind=kLoop, calls=%fused_computation.39 | loop fusion | bytes 589828 | tf_op jit(solution)/shard_map/dynamic_update_slice | solution.py:77
  29.6 1.7 %constant_dynamic-update-slice_fusion.4 = bf16[2304,512]{1,0:T(8,128)(2,1)} fusion(bf16[2304,512]{1,0:T(8,128)(2,1)} %constant_dynamic-update-slice_fusion.5, bf16[288,512]{1,0:T(8,128)(2,1)} %collective-permute-done.12, s32[]{:T(128)S(6)} %select_n.63), kind=kLoop, calls=%fused_computation.38 | loop fusion | bytes 589828 | tf_op jit(solution)/shard_map/dynamic_update_slice | solution.py:77
  31.3 1.7 %constant_dynamic-update-slice_fusion.3 = bf16[2304,512]{1,0:T(8,128)(2,1)} fusion(bf16[2304,512]{1,0:T(8,128)(2,1)} %constant_dynamic-update-slice_fusion.4, bf16[288,512]{1,0:T(8,128)(2,1)} %collective-permute-done.13, s32[]{:T(128)S(6)} %select_n.64), kind=kLoop, calls=%fused_computation.37 | loop fusion | bytes 589828 | tf_op jit(solution)/shard_map/dynamic_update_slice | solution.py:77
  33.8 1.7 %constant_dynamic-update-slice_fusion.1 = bf16[2304,512]{1,0:T(8,128)(2,1)} fusion(bf16[2304,512]{1,0:T(8,128)(2,1)} %constant_dynamic-update-slice_fusion.2, bf16[288,512]{1,0:T(8,128)(2,1)} %collective-permute-done.15, s32[]{:T(128)S(6)} %select_n.66), kind=kLoop, calls=%fused_computation.35 | loop fusion | bytes 589828 | tf_op jit(solution)/shard_map/dynamic_update_slice | solution.py:77
  35.5 2.8 %collective-permute-done.16 = bf16[288,512]{1,0:T(8,128)(2,1)S(1)} collective-permute-done((bf16[288,512]{1,0:T(8,128)(2,1)}, bf16[288,512]{1,0:T(8,128)(2,1)S(1)}, u32[]{:S(2)}, u32[]{:S(2)}) %collective-permute-start.16) | collective-permute-done | bytes 294944 | tf_op jit(solution)/shard_map/ppermute | solution.py:12
  39.0 3.0 %add_convert_fusion = bf16[2304,256]{1,0:T(8,128)(2,1)} fusion(bf16[2304,256]{1,0:T(8,128)(2,1)} %collective-permute-done.1, bf16[256,1024]{1,0:T(8,128)(2,1)S(1)} %copy-done.2, s32[]{:T(128)S(6)} %select_n.59, bf16[256,2304]{1,0:T(8,128)(2,1)S(1)} %copy-done.1, f32[2304]{0:T(1024)S(1)} %copy-done.4, f32[256]{0:T(256)S(1)} %add_rsqrt_fusion), kind=kOutput, calls=%fused_computation.19 | convolution fusion | flops 306118656 | bytes 3683332 | tf_op jit(solution)/shard_map/dot_general | solution.py:56
  44.1 26.6 %collective-permute-done.2 = bf16[2304,256]{1,0:T(8,128)(2,1)} collective-permute-done((bf16[2304,256]{1,0:T(8,128)(2,1)}, bf16[2304,256]{1,0:T(8,128)(2,1)}, u32[]{:S(2)}, u32[]{:S(2)}) %collective-permute-start.2) | collective-permute-done | bytes 1179680 | tf_op jit(solution)/shard_map/ppermute | solution.py:12
  72.3 2.5 %fusion.11 = f32[256,2304]{1,0:T(8,128)S(1)} fusion(bf16[2304,512]{1,0:T(8,128)(2,1)} %collective-permute-done.17, bf16[256,1024]{1,0:T(8,128)(2,1)S(1)} %copy-done.2, s32[]{:T(128)S(6)} %select_n.70), kind=kOutput, calls=%fused_computation.21 | convolution fusion | flops 603979776 | bytes 4980740 | tf_op jit(solution)/shard_map/dot_general | solution.py:82
  74.8 2.7 %fusion.10 = (f32[2304]{0:T(1024)S(1)}, f32[256]{0:T(256)S(1)}, f32[256,2304]{1,0:T(8,128)S(1)}) fusion(bf16[256,2304]{1,0:T(8,128)(2,1)S(1)} %copy-done.1, f32[256]{0:T(256)S(1)} %add_rsqrt_fusion, f32[2304]{0:T(1024)S(1)} %copy-done.4, f32[256,2304]{1,0:T(8,128)S(1)} %fusion.11, bf16[2304,512]{1,0:T(8,128)(2,1)} %constant_dynamic-update-slice_fusion, ...), kind=kOutput, calls=%fused_computation.17 | convolution fusion | flops 608695808 | bytes 8543236 | tf_op jit(solution)/shard_map/dot_general | solution.py:82
  85.8 1.9 %collective-permute-start.24 = (f32[2304]{0:T(1024)S(1)}, f32[2304]{0:T(1024)S(1)}, u32[]{:S(2)}, u32[]{:S(2)}) collective-permute-start(f32[2304]{0:T(1024)S(1)} %add_add_fusion.1), channel_id=1, source_target_pairs={{0,4},{1,5},{2,6},{3,7},{4,0},{5,1},{6,2},{7,3},{8,12},{9,13},{10,... | collective-permute-start | bytes 27656 | tf_op jit(solution)/shard_map/ppermute | solution.py:12
  87.7 2.0 %collective-permute-start.25 = (f32[2304]{0:T(1024)S(1)}, f32[2304]{0:T(1024)S(1)}, u32[]{:S(2)}, u32[]{:S(2)}) collective-permute-start(f32[2304]{0:T(1024)S(1)} %add_add_fusion.1), channel_id=1, source_target_pairs={{0,5},{1,4},{2,7},{3,6},{4,1},{5,0},{6,3},{7,2},{8,13},{9,12},{10,... | collective-permute-start | bytes 27656 | tf_op jit(solution)/shard_map/ppermute | solution.py:12
  91.6 1.7 %fusion.6 = bf16[256,2304]{1,0:T(8,128)(2,1)} fusion(bf16[256,2304]{1,0:T(8,128)(2,1)S(1)} %copy-done.1, f32[256,2304]{1,0:T(8,128)S(1)} %get-tuple-element.36, f32[256]{0:T(256)S(1)} %broadcast_multiply_fusion.1, f32[2304]{0:T(1024)S(1)} %copy-done.4, f32[256]{0:T(256)S(1)} %add_rsqrt_fusion), kind=kLoop, calls=%fused_computation.13 | loop fusion | flops 4718592 | bytes 4729856 | tf_op jit(solution)/shard_map/convert_element_type | solution.py:89
  93.3 3.9 %collective-permute-start.5 = (bf16[288,256]{1,0:T(8,128)(2,1)S(1)}, bf16[288,256]{1,0:T(8,128)(2,1)S(1)}, u32[]{:S(2)}, u32[]{:S(2)}) collective-permute-start(bf16[288,256]{1,0:T(8,128)(2,1)S(1)} %get-tuple-element.33), channel_id=1, source_target_pairs={{0,3},{1,2},{2,1},{3,0},{4,7},{5,6},{6,5},{7,4},{8,11},{9,10},{10,... | collective-permute-start | bytes 442376 | tf_op jit(solution)/shard_map/ppermute | solution.py:12
  97.3 3.1 %collective-permute-start.7 = (bf16[288,256]{1,0:T(8,128)(2,1)S(1)}, bf16[288,256]{1,0:T(8,128)(2,1)S(1)}, u32[]{:S(2)}, u32[]{:S(2)}) collective-permute-start(bf16[288,256]{1,0:T(8,128)(2,1)S(1)} %get-tuple-element.31), channel_id=1, source_target_pairs={{0,5},{1,4},{2,7},{3,6},{4,1},{5,0},{6,3},{7,2},{8,13},{9,12},{10,... | collective-permute-start | bytes 442376 | tf_op jit(solution)/shard_map/ppermute | solution.py:12
  103.1 10.2 %collective-permute-done.6 = bf16[288,256]{1,0:T(8,128)(2,1)S(1)} collective-permute-done((bf16[288,256]{1,0:T(8,128)(2,1)S(1)}, bf16[288,256]{1,0:T(8,128)(2,1)S(1)}, u32[]{:S(2)}, u32[]{:S(2)}) %collective-permute-start.6) | collective-permute-done | bytes 147488 | tf_op jit(solution)/shard_map/ppermute | solution.py:12
  113.3 3.2 %collective-permute-done.7 = bf16[288,256]{1,0:T(8,128)(2,1)S(1)} collective-permute-done((bf16[288,256]{1,0:T(8,128)(2,1)S(1)}, bf16[288,256]{1,0:T(8,128)(2,1)S(1)}, u32[]{:S(2)}, u32[]{:S(2)}) %collective-permute-start.7) | collective-permute-done | bytes 147488 | tf_op jit(solution)/shard_map/ppermute | solution.py:12
  116.4 4.6 %collective-permute-done.8 = bf16[288,256]{1,0:T(8,128)(2,1)S(1)} collective-permute-done((bf16[288,256]{1,0:T(8,128)(2,1)S(1)}, bf16[288,256]{1,0:T(8,128)(2,1)S(1)}, u32[]{:S(2)}, u32[]{:S(2)}) %collective-permute-start.8) | collective-permute-done | bytes 147488 | tf_op jit(solution)/shard_map/ppermute | solution.py:12
  121.0 2.1 %collective-permute-done.9 = bf16[288,256]{1,0:T(8,128)(2,1)S(1)} collective-permute-done((bf16[288,256]{1,0:T(8,128)(2,1)S(1)}, bf16[288,256]{1,0:T(8,128)(2,1)S(1)}, u32[]{:S(2)}, u32[]{:S(2)}) %collective-permute-start.9) | collective-permute-done | bytes 147488 | tf_op jit(solution)/shard_map/ppermute | solution.py:12
  (67 shorter events, 31.2 us)
Async XLA Ops:
  1.7 12.8 %collective-permute-start.11 = (bf16[288,512]{1,0:T(8,128)(2,1)S(1)}, bf16[288,512]{1,0:T(8,128)(2,1)}, u32[]{:S(2)}, u32[]{:S(2)}) collective-permute-start(bf16[288,512]{1,0:T(8,128)(2,1)S(1)} %constant_dynamic-slice_fusion), channel_id=1, source_target_pairs={{0,2},{1,3},{2,0},{3,1},{4,6},{5,7},{6,4},{7,5},{8,10},{9,11},{10,... | collective-permute-start | bytes 884744 | tf_op jit(solution)/shard_map/ppermute | solution.py:12
  1.8 16.3 %collective-permute-start.13 = (bf16[288,512]{1,0:T(8,128)(2,1)S(1)}, bf16[288,512]{1,0:T(8,128)(2,1)}, u32[]{:S(2)}, u32[]{:S(2)}) collective-permute-start(bf16[288,512]{1,0:T(8,128)(2,1)S(1)} %constant_dynamic-slice_fusion), channel_id=1, source_target_pairs={{0,4},{1,5},{2,6},{3,7},{4,0},{5,1},{6,2},{7,3},{8,12},{9,13},{10,... | collective-permute-start | bytes 884744 | tf_op jit(solution)/shard_map/ppermute | solution.py:12
  9.4 29.6 %collective-permute-start.1 = (bf16[2304,256]{1,0:T(8,128)(2,1)}, bf16[2304,256]{1,0:T(8,128)(2,1)}, u32[]{:S(2)}, u32[]{:S(2)}) collective-permute-start(bf16[2304,256]{1,0:T(8,128)(2,1)} %convolution_convert_fusion), channel_id=1, source_target_pairs={{0,8},{8,0},{16,24},{24,16},{1,9},{9,1},{17,25},{25,17},{2,10},{10... | collective-permute-start | bytes 3538952 | tf_op jit(solution)/shard_map/ppermute | solution.py:12
  9.4 12.9 %collective-permute-start.10 = (bf16[288,512]{1,0:T(8,128)(2,1)S(1)}, bf16[288,512]{1,0:T(8,128)(2,1)S(1)}, u32[]{:S(2)}, u32[]{:S(2)}) collective-permute-start(bf16[288,512]{1,0:T(8,128)(2,1)S(1)} %constant_dynamic-slice_fusion), channel_id=1, source_target_pairs={{0,1},{1,0},{2,3},{3,2},{4,5},{5,4},{6,7},{7,6},{8,9},{9,8},{10,11... | collective-permute-start | bytes 884744 | tf_op jit(solution)/shard_map/ppermute | solution.py:12
  14.6 15.0 %collective-permute-start.12 = (bf16[288,512]{1,0:T(8,128)(2,1)}, bf16[288,512]{1,0:T(8,128)(2,1)}, u32[]{:S(2)}, u32[]{:S(2)}) collective-permute-start(bf16[288,512]{1,0:T(8,128)(2,1)} %collective-permute-done.11), channel_id=1, source_target_pairs={{0,1},{1,0},{2,3},{3,2},{4,5},{5,4},{6,7},{7,6},{8,9},{9,8},{10,11... | collective-permute-start | bytes 884744 | tf_op jit(solution)/shard_map/ppermute | solution.py:12
  18.1 10.8 %collective-permute-start.15 = (bf16[288,512]{1,0:T(8,128)(2,1)}, bf16[288,512]{1,0:T(8,128)(2,1)}, u32[]{:S(2)}, u32[]{:S(2)}) collective-permute-start(bf16[288,512]{1,0:T(8,128)(2,1)} %collective-permute-done.13), channel_id=1, source_target_pairs={{0,2},{1,3},{2,0},{3,1},{4,6},{5,7},{6,4},{7,5},{8,10},{9,11},{10,... | collective-permute-start | bytes 884744 | tf_op jit(solution)/shard_map/ppermute | solution.py:12
  22.2 21.8 %collective-permute-start = (bf16[2304,256]{1,0:T(8,128)(2,1)}, bf16[2304,256]{1,0:T(8,128)(2,1)S(1)}, u32[]{:S(2)}, u32[]{:S(2)}) collective-permute-start(bf16[2304,256]{1,0:T(8,128)(2,1)} %convolution_convert_fusion.1), channel_id=1, source_target_pairs={{0,8},{8,0},{16,24},{24,16},{1,9},{9,1},{17,25},{25,17},{2,10},{10... | collective-permute-start | bytes 3538952 | tf_op jit(solution)/shard_map/ppermute | solution.py:12
  22.3 10.8 %collective-permute-start.14 = (bf16[288,512]{1,0:T(8,128)(2,1)}, bf16[288,512]{1,0:T(8,128)(2,1)S(1)}, u32[]{:S(2)}, u32[]{:S(2)}) collective-permute-start(bf16[288,512]{1,0:T(8,128)(2,1)} %collective-permute-done.13), channel_id=1, source_target_pairs={{0,1},{1,0},{2,3},{3,2},{4,5},{5,4},{6,7},{7,6},{8,9},{9,8},{10,11... | collective-permute-start | bytes 884744 | tf_op jit(solution)/shard_map/ppermute | solution.py:12
  28.9 9.3 %collective-permute-start.16 = (bf16[288,512]{1,0:T(8,128)(2,1)}, bf16[288,512]{1,0:T(8,128)(2,1)S(1)}, u32[]{:S(2)}, u32[]{:S(2)}) collective-permute-start(bf16[288,512]{1,0:T(8,128)(2,1)} %collective-permute-done.15), channel_id=1, source_target_pairs={{0,1},{1,0},{2,3},{3,2},{4,5},{5,4},{6,7},{7,6},{8,9},{9,8},{10,11... | collective-permute-start | bytes 884744 | tf_op jit(solution)/shard_map/ppermute | solution.py:12
  39.0 33.3 %collective-permute-start.17 = (bf16[2304,512]{1,0:T(8,128)(2,1)}, bf16[2304,512]{1,0:T(8,128)(2,1)}, u32[]{:S(2)}, u32[]{:S(2)}) collective-permute-start(bf16[2304,512]{1,0:T(8,128)(2,1)} %constant_dynamic-update-slice_fusion), channel_id=1, source_target_pairs={{0,8},{8,0},{16,24},{24,16},{1,9},{9,1},{17,25},{25,17},{2,10},{10... | collective-permute-start | bytes 7077896 | tf_op jit(solution)/shard_map/ppermute | solution.py:12
  42.0 28.7 %collective-permute-start.2 = (bf16[2304,256]{1,0:T(8,128)(2,1)}, bf16[2304,256]{1,0:T(8,128)(2,1)}, u32[]{:S(2)}, u32[]{:S(2)}) collective-permute-start(bf16[2304,256]{1,0:T(8,128)(2,1)} %add_convert_fusion), channel_id=1, source_target_pairs={{0,16},{8,24},{16,0},{24,8},{1,17},{9,25},{17,1},{25,9},{2,18},{10... | collective-permute-start | bytes 3538952 | tf_op jit(solution)/shard_map/ppermute | solution.py:12
  81.0 6.7 %collective-permute-start.4 = (bf16[288,256]{1,0:T(8,128)(2,1)S(1)}, bf16[288,256]{1,0:T(8,128)(2,1)S(1)}, u32[]{:S(2)}, u32[]{:S(2)}) collective-permute-start(bf16[288,256]{1,0:T(8,128)(2,1)S(1)} %get-tuple-element.34), channel_id=1, source_target_pairs={{0,2},{1,3},{2,0},{3,1},{4,6},{5,7},{6,4},{7,5},{8,10},{9,11},{10,... | collective-permute-start | bytes 442376 | tf_op jit(solution)/shard_map/ppermute | solution.py:12
  82.2 7.4 %collective-permute-start.21 = (f32[2304]{0:T(1024)S(1)}, f32[2304]{0:T(1024)S(1)}, u32[]{:S(2)}, u32[]{:S(2)}) collective-permute-start(f32[2304]{0:T(1024)S(1)} %add_add_fusion.1), channel_id=1, source_target_pairs={{0,1},{1,0},{2,3},{3,2},{4,5},{5,4},{6,7},{7,6},{8,9},{9,8},{10,11... | collective-permute-start | bytes 27656 | tf_op jit(solution)/shard_map/ppermute | solution.py:12
  83.7 7.5 %collective-permute-start.22 = (f32[2304]{0:T(1024)S(1)}, f32[2304]{0:T(1024)S(1)}, u32[]{:S(2)}, u32[]{:S(2)}) collective-permute-start(f32[2304]{0:T(1024)S(1)} %add_add_fusion.1), channel_id=1, source_target_pairs={{0,2},{1,3},{2,0},{3,1},{4,6},{5,7},{6,4},{7,5},{8,10},{9,11},{10,... | collective-permute-start | bytes 27656 | tf_op jit(solution)/shard_map/ppermute | solution.py:12
  84.9 8.5 %collective-permute-start.23 = (f32[2304]{0:T(1024)S(1)}, f32[2304]{0:T(1024)S(1)}, u32[]{:S(2)}, u32[]{:S(2)}) collective-permute-start(f32[2304]{0:T(1024)S(1)} %add_add_fusion.1), channel_id=1, source_target_pairs={{0,3},{1,2},{2,1},{3,0},{4,7},{5,6},{6,5},{7,4},{8,11},{9,10},{10,... | collective-permute-start | bytes 27656 | tf_op jit(solution)/shard_map/ppermute | solution.py:12
  85.8 11.5 %collective-permute-start.24 = (f32[2304]{0:T(1024)S(1)}, f32[2304]{0:T(1024)S(1)}, u32[]{:S(2)}, u32[]{:S(2)}) collective-permute-start(f32[2304]{0:T(1024)S(1)} %add_add_fusion.1), channel_id=1, source_target_pairs={{0,4},{1,5},{2,6},{3,7},{4,0},{5,1},{6,2},{7,3},{8,12},{9,13},{10,... | collective-permute-start | bytes 27656 | tf_op jit(solution)/shard_map/ppermute | solution.py:12
  87.7 9.7 %collective-permute-start.25 = (f32[2304]{0:T(1024)S(1)}, f32[2304]{0:T(1024)S(1)}, u32[]{:S(2)}, u32[]{:S(2)}) collective-permute-start(f32[2304]{0:T(1024)S(1)} %add_add_fusion.1), channel_id=1, source_target_pairs={{0,5},{1,4},{2,7},{3,6},{4,1},{5,0},{6,3},{7,2},{8,13},{9,12},{10,... | collective-permute-start | bytes 27656 | tf_op jit(solution)/shard_map/ppermute | solution.py:12
  89.6 10.8 %collective-permute-start.26 = (f32[2304]{0:T(1024)S(1)}, f32[2304]{0:T(1024)S(1)}, u32[]{:S(2)}, u32[]{:S(2)}) collective-permute-start(f32[2304]{0:T(1024)S(1)} %add_add_fusion.1), channel_id=1, source_target_pairs={{0,6},{1,7},{2,4},{3,5},{4,2},{5,3},{6,0},{7,1},{8,14},{9,15},{10,... | collective-permute-start | bytes 27656 | tf_op jit(solution)/shard_map/ppermute | solution.py:12
  91.2 10.2 %collective-permute-start.27 = (f32[2304]{0:T(1024)S(1)}, f32[2304]{0:T(1024)S(1)}, u32[]{:S(2)}, u32[]{:S(2)}) collective-permute-start(f32[2304]{0:T(1024)S(1)} %add_add_fusion.1), channel_id=1, source_target_pairs={{0,7},{1,6},{2,5},{3,4},{4,3},{5,2},{6,1},{7,0},{8,15},{9,14},{10,... | collective-permute-start | bytes 27656 | tf_op jit(solution)/shard_map/ppermute | solution.py:12
  93.3 9.8 %collective-permute-start.5 = (bf16[288,256]{1,0:T(8,128)(2,1)S(1)}, bf16[288,256]{1,0:T(8,128)(2,1)S(1)}, u32[]{:S(2)}, u32[]{:S(2)}) collective-permute-start(bf16[288,256]{1,0:T(8,128)(2,1)S(1)} %get-tuple-element.33), channel_id=1, source_target_pairs={{0,3},{1,2},{2,1},{3,0},{4,7},{5,6},{6,5},{7,4},{8,11},{9,10},{10,... | collective-permute-start | bytes 442376 | tf_op jit(solution)/shard_map/ppermute | solution.py:12
  97.2 16.0 %collective-permute-start.6 = (bf16[288,256]{1,0:T(8,128)(2,1)S(1)}, bf16[288,256]{1,0:T(8,128)(2,1)S(1)}, u32[]{:S(2)}, u32[]{:S(2)}) collective-permute-start(bf16[288,256]{1,0:T(8,128)(2,1)S(1)} %get-tuple-element.32), channel_id=1, source_target_pairs={{0,4},{1,5},{2,6},{3,7},{4,0},{5,1},{6,2},{7,3},{8,12},{9,13},{10,... | collective-permute-start | bytes 442376 | tf_op jit(solution)/shard_map/ppermute | solution.py:12
  97.3 19.1 %collective-permute-start.7 = (bf16[288,256]{1,0:T(8,128)(2,1)S(1)}, bf16[288,256]{1,0:T(8,128)(2,1)S(1)}, u32[]{:S(2)}, u32[]{:S(2)}) collective-permute-start(bf16[288,256]{1,0:T(8,128)(2,1)S(1)} %get-tuple-element.31), channel_id=1, source_target_pairs={{0,5},{1,4},{2,7},{3,6},{4,1},{5,0},{6,3},{7,2},{8,13},{9,12},{10,... | collective-permute-start | bytes 442376 | tf_op jit(solution)/shard_map/ppermute | solution.py:12
  100.5 20.6 %collective-permute-start.8 = (bf16[288,256]{1,0:T(8,128)(2,1)S(1)}, bf16[288,256]{1,0:T(8,128)(2,1)S(1)}, u32[]{:S(2)}, u32[]{:S(2)}) collective-permute-start(bf16[288,256]{1,0:T(8,128)(2,1)S(1)} %get-tuple-element.30), channel_id=1, source_target_pairs={{0,6},{1,7},{2,4},{3,5},{4,2},{5,3},{6,0},{7,1},{8,14},{9,15},{10,... | collective-permute-start | bytes 442376 | tf_op jit(solution)/shard_map/ppermute | solution.py:12
  101.4 21.6 %collective-permute-start.9 = (bf16[288,256]{1,0:T(8,128)(2,1)S(1)}, bf16[288,256]{1,0:T(8,128)(2,1)S(1)}, u32[]{:S(2)}, u32[]{:S(2)}) collective-permute-start(bf16[288,256]{1,0:T(8,128)(2,1)S(1)} %get-tuple-element.29), channel_id=1, source_target_pairs={{0,7},{1,6},{2,5},{3,4},{4,3},{5,2},{6,1},{7,0},{8,15},{9,14},{10,... | collective-permute-start | bytes 442376 | tf_op jit(solution)/shard_map/ppermute | solution.py:12
  (9 other events, 70.8 us)

commit v2 on v1

--- a/solution.py
+++ b/solution.py
@@ -58,17 +58,30 @@
     crossing = {}
     for flip in list(range(2, n_rep, 2)) + [0]:
         crossing[flip] = swap(partial(flip + 1).astype(bf16), "rep", 1)
-    sent = {}
+
+    def side(value, flip):
+        blocks = value.reshape(n_grp // 2, 2, rows, cols)
+        return lax.dynamic_index_in_dim(blocks, (grp % 2) ^ flip, 1, keepdims=False)
+
+    sent = {0: [], 1: []}
     for flip in range(2, n_rep, 2):
-        sent[flip] = swap((partial(flip) + crossing[flip].astype(f32)).astype(bf16), "rep", flip)
-    section = partial(0) + crossing[0].astype(f32)
-    for flip in sent:
-        section = section + sent[flip].astype(f32)
-    narrow = section.astype(bf16)
-    weight_sum = lax.dynamic_slice_in_dim(section, grp * rows, rows, 0)
+        summed = (partial(flip) + crossing[flip].astype(f32)).astype(bf16)
+        sent[1].append(swap(side(summed, 1), "rep", flip))
+        sent[0].append(swap(side(summed, 0), "rep", flip))
+    local = partial(0) + crossing[0].astype(f32)
+    sections, narrow = {}, {}
+    for y_flip in (1, 0):
+        if y_flip == 0 and sent[0]:
+            sent[0][0], _ = lax.optimization_barrier((sent[0][0], narrow[1]))
+        sections[y_flip] = side(local, y_flip)
+        for block in sent[y_flip]:
+            sections[y_flip] = sections[y_flip] + block.astype(f32)
+        narrow[y_flip] = sections[y_flip].astype(bf16)
+    pieces[n_grp - 1], _ = lax.optimization_barrier((pieces[n_grp - 1], narrow[1]))
+    weight_sum = lax.dynamic_index_in_dim(sections[0], grp // 2, 0, keepdims=False)
     arriving = []
-    for flip in range(1, n_grp):
-        block = lax.dynamic_slice_in_dim(narrow, (grp ^ flip) * rows, rows, 0)
+    for flip in list(range(1, n_grp, 2)) + list(range(2, n_grp, 2)):
+        block = lax.dynamic_index_in_dim(narrow[flip % 2], (grp ^ flip) // 2, 0, keepdims=False)
         arriving.append(swap(block, "grp", flip))
 
     canvas, pieces[1] = lax.optimization_barrier((own, pieces[1]))

time: 125 us -> 119 us (0.952)
  the two profiles are of different devices: /device:TPU:8 before, /device:TPU:0 now
where the time goes in v2:
time: 119 us; the launch traced here: 118 us
  waiting for transfers between devices  47.6 us (40%)
  starting transfers between devices  38.2 us (32%)
  matrix products  13.4 us (11%)
  local copies, waits for them, and re-layouts  11.7 us (10%)
  other arithmetic  6.54 us (5%)
    ppermute x29, waiting for transfers between devices, swap(): return lax.ppermute(value, axis, [(i, i ^ flip) for i in range(size)])  47.6 us
    ppermute x29, starting transfers between devices, swap(): return lax.ppermute(value, axis, [(i, i ^ flip) for i in range(size)])  38.2 us
    dynamic_update_slice x7, local copies, waits for them, and re-layouts, shards(): lax.dynamic_update_slice_in_dim(gathered, pieces[flip], (grp ^ flip) * ro...  8.97 us
    dot_general x4, matrix products, partial(): lax.dot_general(normed, block, (((0,), (0,)), ((), ())), preferred_elemen...  8.12 us
    dot_general x2, matrix products, back(): lax.dot_general(block, weight, (((1,), (1,)), ((), ())), preferred_elemen...  5.26 us
  transfers between devices with their start and end apart: 29, of which 8 were waited for; matrix products, arithmetic and copies ran while one was open for 21% of the time, Pallas kernels for 0%

profile of v2, /device:TPU:0, one launch (start us, length us, event | category | flops | bytes accessed | tf_op | source)
XLA Modules:
  0.0 118.1 jit_solution(13211158909950131644)
XLA Ops:
  0.7 1.7 %fusion.7 = f32[256]{0:T(256)S(1)} fusion(bf16[256,2304]{1,0:T(8,128)(2,1)} %param.4), kind=kLoop, calls=%fused_computation.14 | loop fusion | flops 1769216 | bytes 1180672 | tf_op jit(solution)/shard_map/reduce_sum | solution.py:51
  2.4 2.9 %convolution_convert_fusion = bf16[2304,256]{1,0:T(8,128)(2,1)} fusion(bf16[256,1024]{1,0:T(8,128)(2,1)} %param.7, s32[]{:T(128)S(6)} %select_n.123, bf16[256,2304]{1,0:T(8,128)(2,1)} %param.4, f32[2304]{0:T(1024)} %param.5, f32[256]{0:T(256)S(1)} %add_rsqrt_fusion), kind=kOutput, calls=%fused_computation.5 | convolution fusion | flops 304939008 | bytes 2503684 | tf_op jit(solution)/shard_map/dot_general | solution.py:56
  5.9 3.6 %collective-permute-start.14 = (bf16[288,512]{1,0:T(8,128)(2,1)S(1)}, bf16[288,512]{1,0:T(8,128)(2,1)}, u32[]{:S(2)}, u32[]{:S(2)}) collective-permute-start(bf16[288,512]{1,0:T(8,128)(2,1)S(1)} %constant_dynamic-slice_fusion), channel_id=1, source_target_pairs={{0,4},{1,5},{2,6},{3,7},{4,0},{5,1},{6,2},{7,3},{8,12},{9,13},{10,... | collective-permute-start | bytes 884744 | tf_op jit(solution)/shard_map/ppermute | solution.py:12
  12.6 11.1 %collective-permute-done.14 = bf16[288,512]{1,0:T(8,128)(2,1)} collective-permute-done((bf16[288,512]{1,0:T(8,128)(2,1)S(1)}, bf16[288,512]{1,0:T(8,128)(2,1)}, u32[]{:S(2)}, u32[]{:S(2)}) %collective-permute-start.14) | collective-permute-done | bytes 294944 | tf_op jit(solution)/shard_map/ppermute | solution.py:12
  25.8 2.5 %convolution_convert_fusion.1 = bf16[2304,256]{1,0:T(8,128)(2,1)} fusion(bf16[256,1024]{1,0:T(8,128)(2,1)} %param.7, s32[]{:T(128)S(6)} %select_n.119, bf16[256,2304]{1,0:T(8,128)(2,1)S(1)} %copy-done.1, f32[2304]{0:T(1024)S(1)} %copy-done.5, f32[256]{0:T(256)S(1)} %add_rsqrt_fusion), kind=kOutput, calls=%fused_computation.6 | convolution fusion | flops 304939008 | bytes 2500612 | tf_op jit(solution)/shard_map/dot_general | solution.py:56
  28.9 1.7 %tile.4 = bf16[8,288,512]{2,1,0:T(8,128)(2,1)} broadcast(bf16[288,512]{1,0:T(8,128)(2,1)S(1)} %constant_dynamic-slice_fusion), dimensions={1,2} | broadcast | bytes 2654208 | tf_op jit(solution)/shard_map/tile | solution.py:88
  30.6 1.7 %constant_dynamic-update-slice_fusion.6 = bf16[2304,512]{1,0:T(8,128)(2,1)} fusion(bf16[2304,512]{1,0:T(8,128)(2,1)} %bitcast.13, bf16[288,512]{1,0:T(8,128)(2,1)} %collective-permute-done.11, s32[]{:T(128)S(6)} %select_n.141), kind=kLoop, calls=%fused_computation.58 | loop fusion | bytes 589828 | tf_op jit(solution)/shard_map/dynamic_update_slice | solution.py:90
  32.2 1.7 %constant_dynamic-update-slice_fusion.5 = bf16[2304,512]{1,0:T(8,128)(2,1)} fusion(bf16[2304,512]{1,0:T(8,128)(2,1)} %constant_dynamic-update-slice_fusion.6, bf16[288,512]{1,0:T(8,128)(2,1)} %collective-permute-done.12, s32[]{:T(128)S(6)} %select_n.142), kind=kLoop, calls=%fused_computation.57 | loop fusion | bytes 589828 | tf_op jit(solution)/shard_map/dynamic_update_slice | solution.py:90
  35.5 1.7 %constant_dynamic-update-slice_fusion.4 = bf16[2304,512]{1,0:T(8,128)(2,1)} fusion(bf16[2304,512]{1,0:T(8,128)(2,1)} %constant_dynamic-update-slice_fusion.5, bf16[288,512]{1,0:T(8,128)(2,1)} %collective-permute-done.13, s32[]{:T(128)S(6)} %select_n.143), kind=kLoop, calls=%fused_computation.56 | loop fusion | bytes 589828 | tf_op jit(solution)/shard_map/dynamic_update_slice | solution.py:90
  37.2 2.0 %add_convert_fusion = bf16[2304,256]{1,0:T(8,128)(2,1)S(1)} fusion(bf16[2304,256]{1,0:T(8,128)(2,1)} %collective-permute-done.1, bf16[256,1024]{1,0:T(8,128)(2,1)S(1)} %copy-done.3, s32[]{:T(128)S(6)} %select_n.122, bf16[256,2304]{1,0:T(8,128)(2,1)S(1)} %copy-done.1, f32[2304]{0:T(1024)S(1)} %copy-done.5, f32[256]{0:T(256)S(1)} %add_rsqrt_fusion), kind=kOutput, calls=%fused_computation.18 | convolution fusion | flops 306118656 | bytes 3683332 | tf_op jit(solution)/shard_map/dot_general | solution.py:56
  41.5 1.7 %constant_dynamic-update-slice_fusion.3 = bf16[2304,512]{1,0:T(8,128)(2,1)} fusion(bf16[2304,512]{1,0:T(8,128)(2,1)} %constant_dynamic-update-slice_fusion.4, bf16[288,512]{1,0:T(8,128)(2,1)} %collective-permute-done.14, s32[]{:T(128)S(6)} %select_n.144), kind=kLoop, calls=%fused_computation.55 | loop fusion | bytes 589828 | tf_op jit(solution)/shard_map/dynamic_update_slice | solution.py:90
  45.4 9.8 %collective-permute-done.2 = bf16[4,288,256]{2,1,0:T(8,128)(2,1)S(1)} collective-permute-done((bf16[4,288,256]{2,1,0:T(8,128)(2,1)S(1)}, bf16[4,288,256]{2,1,0:T(8,128)(2,1)S(1)}, u32[]{:S(2)}, u32[]{:S(2)}) %collective-permute-start.2) | collective-permute-done | bytes 589856 | tf_op jit(solution)/shard_map/ppermute | solution.py:12
  57.6 14.5 %collective-permute-done.7 = bf16[4,288,256]{2,1,0:T(8,128)(2,1)S(1)} collective-permute-done((bf16[4,288,256]{2,1,0:T(8,128)(2,1)}, bf16[4,288,256]{2,1,0:T(8,128)(2,1)S(1)}, u32[]{:S(2)}, u32[]{:S(2)}) %collective-permute-start.7) | collective-permute-done | bytes 589856 | tf_op jit(solution)/shard_map/ppermute | solution.py:12
  73.5 2.9 %collective-permute-start.10 = (bf16[288,256]{1,0:T(8,128)(2,1)S(1)}, bf16[288,256]{1,0:T(8,128)(2,1)S(1)}, u32[]{:S(2)}, u32[]{:S(2)}) collective-permute-start(bf16[288,256]{1,0:T(8,128)(2,1)S(1)} %get-tuple-element.35), channel_id=1, source_target_pairs={{0,6},{1,7},{2,4},{3,5},{4,2},{5,3},{6,0},{7,1},{8,14},{9,15},{10,... | collective-permute-start | bytes 442376 | tf_op jit(solution)/shard_map/ppermute | solution.py:12
  77.1 2.5 %fusion.19 = f32[256,2304]{1,0:T(8,128)S(1)} fusion(bf16[2304,512]{1,0:T(8,128)(2,1)} %collective-permute-done.18, bf16[256,1024]{1,0:T(8,128)(2,1)S(1)} %copy-done.4, s32[]{:T(128)S(6)} %select_n.148), kind=kOutput, calls=%fused_computation.33 | convolution fusion | flops 603979776 | bytes 4980740 | tf_op jit(solution)/shard_map/dot_general | solution.py:95
  79.6 2.8 %fusion.10 = (f32[2304]{0:T(1024)S(1)}, f32[256]{0:T(256)S(1)}, f32[256,2304]{1,0:T(8,128)S(1)}) fusion(bf16[256,2304]{1,0:T(8,128)(2,1)S(1)} %copy-done.1, f32[256]{0:T(256)S(1)} %add_rsqrt_fusion, f32[2304]{0:T(1024)S(1)} %copy-done.5, f32[256,2304]{1,0:T(8,128)S(1)} %fusion.19, bf16[2304,512]{1,0:T(8,128)(2,1)} %constant_dynamic-update-slice_fusion, ...), kind=kOutput, calls=%fused_computation.17 | convolution fusion | flops 608695808 | bytes 8543236 | tf_op jit(solution)/shard_map/dot_general | solution.py:95
  86.6 2.5 %collective-permute-start.28 = (f32[2304]{0:T(1024)S(1)}, f32[2304]{0:T(1024)S(1)}, u32[]{:S(2)}, u32[]{:S(2)}) collective-permute-start(f32[2304]{0:T(1024)S(1)} %add_add_fusion.1), channel_id=1, source_target_pairs={{0,7},{1,6},{2,5},{3,4},{4,3},{5,2},{6,1},{7,0},{8,15},{9,14},{10,... | collective-permute-start | bytes 27656 | tf_op jit(solution)/shard_map/ppermute | solution.py:12
  91.6 2.7 %collective-permute-start.25 = (f32[2304]{0:T(1024)S(1)}, f32[2304]{0:T(1024)S(1)}, u32[]{:S(2)}, u32[]{:S(2)}) collective-permute-start(f32[2304]{0:T(1024)S(1)} %add_add_fusion.1), channel_id=1, source_target_pairs={{0,4},{1,5},{2,6},{3,7},{4,0},{5,1},{6,2},{7,3},{8,12},{9,13},{10,... | collective-permute-start | bytes 27656 | tf_op jit(solution)/shard_map/ppermute | solution.py:12
  94.7 1.7 %collective-permute-start.23 = (f32[2304]{0:T(1024)S(1)}, f32[2304]{0:T(1024)S(1)}, u32[]{:S(2)}, u32[]{:S(2)}) collective-permute-start(f32[2304]{0:T(1024)S(1)} %add_add_fusion.1), channel_id=1, source_target_pairs={{0,2},{1,3},{2,0},{3,1},{4,6},{5,7},{6,4},{7,5},{8,10},{9,11},{10,... | collective-permute-start | bytes 27656 | tf_op jit(solution)/shard_map/ppermute | solution.py:12
  97.9 1.7 %fusion.6 = bf16[256,2304]{1,0:T(8,128)(2,1)} fusion(bf16[256,2304]{1,0:T(8,128)(2,1)S(1)} %copy-done.1, f32[256,2304]{1,0:T(8,128)S(1)} %get-tuple-element.42, f32[256]{0:T(256)S(1)} %broadcast_multiply_fusion.1, f32[2304]{0:T(1024)S(1)} %copy-done.5, f32[256]{0:T(256)S(1)} %add_rsqrt_fusion), kind=kLoop, calls=%fused_computation.13 | loop fusion | flops 4718592 | bytes 4729856 | tf_op jit(solution)/shard_map/convert_element_type | solution.py:102
  99.9 2.4 %collective-permute-start.6 = (bf16[288,256]{1,0:T(8,128)(2,1)S(1)}, bf16[288,256]{1,0:T(8,128)(2,1)S(1)}, u32[]{:S(2)}, u32[]{:S(2)}) collective-permute-start(bf16[288,256]{1,0:T(8,128)(2,1)S(1)} %get-tuple-element.38), channel_id=1, source_target_pairs={{0,7},{1,6},{2,5},{3,4},{4,3},{5,2},{6,1},{7,0},{8,15},{9,14},{10,... | collective-permute-start | bytes 442376 | tf_op jit(solution)/shard_map/ppermute | solution.py:12
  102.2 1.7 %collective-permute-start.5 = (bf16[288,256]{1,0:T(8,128)(2,1)S(1)}, bf16[288,256]{1,0:T(8,128)(2,1)S(1)}, u32[]{:S(2)}, u32[]{:S(2)}) collective-permute-start(bf16[288,256]{1,0:T(8,128)(2,1)S(1)} %get-tuple-element.39), channel_id=1, source_target_pairs={{0,5},{1,4},{2,7},{3,6},{4,1},{5,0},{6,3},{7,2},{8,13},{9,12},{10,... | collective-permute-start | bytes 442376 | tf_op jit(solution)/shard_map/ppermute | solution.py:12
  106.6 3.7 %collective-permute-done.8 = bf16[288,256]{1,0:T(8,128)(2,1)S(1)} collective-permute-done((bf16[288,256]{1,0:T(8,128)(2,1)S(1)}, bf16[288,256]{1,0:T(8,128)(2,1)S(1)}, u32[]{:S(2)}, u32[]{:S(2)}) %collective-permute-start.8) | collective-permute-done | bytes 147488 | tf_op jit(solution)/shard_map/ppermute | solution.py:12
  110.3 5.1 %collective-permute-done.5 = bf16[288,256]{1,0:T(8,128)(2,1)S(1)} collective-permute-done((bf16[288,256]{1,0:T(8,128)(2,1)S(1)}, bf16[288,256]{1,0:T(8,128)(2,1)S(1)}, u32[]{:S(2)}, u32[]{:S(2)}) %collective-permute-start.5) | collective-permute-done | bytes 147488 | tf_op jit(solution)/shard_map/ppermute | solution.py:12
  (74 shorter events, 31.1 us)
Async XLA Ops:
  5.3 31.8 %collective-permute-start.1 = (bf16[2304,256]{1,0:T(8,128)(2,1)}, bf16[2304,256]{1,0:T(8,128)(2,1)}, u32[]{:S(2)}, u32[]{:S(2)}) collective-permute-start(bf16[2304,256]{1,0:T(8,128)(2,1)} %convolution_convert_fusion), channel_id=1, source_target_pairs={{0,8},{8,0},{16,24},{24,16},{1,9},{9,1},{17,25},{25,17},{2,10},{10... | collective-permute-start | bytes 3538952 | tf_op jit(solution)/shard_map/ppermute | solution.py:12
  5.9 17.8 %collective-permute-start.14 = (bf16[288,512]{1,0:T(8,128)(2,1)S(1)}, bf16[288,512]{1,0:T(8,128)(2,1)}, u32[]{:S(2)}, u32[]{:S(2)}) collective-permute-start(bf16[288,512]{1,0:T(8,128)(2,1)S(1)} %constant_dynamic-slice_fusion), channel_id=1, source_target_pairs={{0,4},{1,5},{2,6},{3,7},{4,0},{5,1},{6,2},{7,3},{8,12},{9,13},{10,... | collective-permute-start | bytes 884744 | tf_op jit(solution)/shard_map/ppermute | solution.py:12
  9.5 14.7 %collective-permute-start.12 = (bf16[288,512]{1,0:T(8,128)(2,1)S(1)}, bf16[288,512]{1,0:T(8,128)(2,1)}, u32[]{:S(2)}, u32[]{:S(2)}) collective-permute-start(bf16[288,512]{1,0:T(8,128)(2,1)S(1)} %constant_dynamic-slice_fusion), channel_id=1, source_target_pairs={{0,2},{1,3},{2,0},{3,1},{4,6},{5,7},{6,4},{7,5},{8,10},{9,11},{10,... | collective-permute-start | bytes 884744 | tf_op jit(solution)/shard_map/ppermute | solution.py:12
  11.1 17.3 %collective-permute-start.11 = (bf16[288,512]{1,0:T(8,128)(2,1)S(1)}, bf16[288,512]{1,0:T(8,128)(2,1)}, u32[]{:S(2)}, u32[]{:S(2)}) collective-permute-start(bf16[288,512]{1,0:T(8,128)(2,1)S(1)} %constant_dynamic-slice_fusion), channel_id=1, source_target_pairs={{0,1},{1,0},{2,3},{3,2},{4,5},{5,4},{6,7},{7,6},{8,9},{9,8},{10,11... | collective-permute-start | bytes 884744 | tf_op jit(solution)/shard_map/ppermute | solution.py:12
  23.7 10.2 %collective-permute-start.16 = (bf16[288,512]{1,0:T(8,128)(2,1)}, bf16[288,512]{1,0:T(8,128)(2,1)S(1)}, u32[]{:S(2)}, u32[]{:S(2)}) collective-permute-start(bf16[288,512]{1,0:T(8,128)(2,1)} %collective-permute-done.14), channel_id=1, source_target_pairs={{0,2},{1,3},{2,0},{3,1},{4,6},{5,7},{6,4},{7,5},{8,10},{9,11},{10,... | collective-permute-start | bytes 884744 | tf_op jit(solution)/shard_map/ppermute | solution.py:12
  24.2 11.2 %collective-permute-start.13 = (bf16[288,512]{1,0:T(8,128)(2,1)}, bf16[288,512]{1,0:T(8,128)(2,1)}, u32[]{:S(2)}, u32[]{:S(2)}) collective-permute-start(bf16[288,512]{1,0:T(8,128)(2,1)} %collective-permute-done.12), channel_id=1, source_target_pairs={{0,1},{1,0},{2,3},{3,2},{4,5},{5,4},{6,7},{7,6},{8,9},{9,8},{10,11... | collective-permute-start | bytes 884744 | tf_op jit(solution)/shard_map/ppermute | solution.py:12
  28.3 16.4 %collective-permute-start = (bf16[2304,256]{1,0:T(8,128)(2,1)}, bf16[2304,256]{1,0:T(8,128)(2,1)S(1)}, u32[]{:S(2)}, u32[]{:S(2)}) collective-permute-start(bf16[2304,256]{1,0:T(8,128)(2,1)} %convolution_convert_fusion.1), channel_id=1, source_target_pairs={{0,8},{8,0},{16,24},{24,16},{1,9},{9,1},{17,25},{25,17},{2,10},{10... | collective-permute-start | bytes 3538952 | tf_op jit(solution)/shard_map/ppermute | solution.py:12
  28.3 14.9 %collective-permute-start.15 = (bf16[288,512]{1,0:T(8,128)(2,1)}, bf16[288,512]{1,0:T(8,128)(2,1)S(1)}, u32[]{:S(2)}, u32[]{:S(2)}) collective-permute-start(bf16[288,512]{1,0:T(8,128)(2,1)} %collective-permute-done.14), channel_id=1, source_target_pairs={{0,1},{1,0},{2,3},{3,2},{4,5},{5,4},{6,7},{7,6},{8,9},{9,8},{10,11... | collective-permute-start | bytes 884744 | tf_op jit(solution)/shard_map/ppermute | solution.py:12
  33.9 21.4 %collective-permute-start.17 = (bf16[288,512]{1,0:T(8,128)(2,1)S(1)}, bf16[288,512]{1,0:T(8,128)(2,1)S(1)}, u32[]{:S(2)}, u32[]{:S(2)}) collective-permute-start(bf16[288,512]{1,0:T(8,128)(2,1)S(1)} %collective-permute-done.16), channel_id=1, source_target_pairs={{0,1},{1,0},{2,3},{3,2},{4,5},{5,4},{6,7},{7,6},{8,9},{9,8},{10,11... | collective-permute-start | bytes 884744 | tf_op jit(solution)/shard_map/ppermute | solution.py:12
  40.0 15.1 %collective-permute-start.2 = (bf16[4,288,256]{2,1,0:T(8,128)(2,1)S(1)}, bf16[4,288,256]{2,1,0:T(8,128)(2,1)S(1)}, u32[]{:S(2)}, u32[]{:S(2)}) collective-permute-start(bf16[4,288,256]{2,1,0:T(8,128)(2,1)S(1)} %get-tuple-element.34), channel_id=1, source_target_pairs={{0,16},{8,24},{16,0},{24,8},{1,17},{9,25},{17,1},{25,9},{2,18},{10... | collective-permute-start | bytes 1769480 | tf_op jit(solution)/shard_map/ppermute | solution.py:12
  56.1 21.0 %collective-permute-start.18 = (bf16[2304,512]{1,0:T(8,128)(2,1)}, bf16[2304,512]{1,0:T(8,128)(2,1)}, u32[]{:S(2)}, u32[]{:S(2)}) collective-permute-start(bf16[2304,512]{1,0:T(8,128)(2,1)} %constant_dynamic-update-slice_fusion), channel_id=1, source_target_pairs={{0,8},{8,0},{16,24},{24,16},{1,9},{9,1},{17,25},{25,17},{2,10},{10... | collective-permute-start | bytes 7077896 | tf_op jit(solution)/shard_map/ppermute | solution.py:12
  56.1 16.0 %collective-permute-start.7 = (bf16[4,288,256]{2,1,0:T(8,128)(2,1)}, bf16[4,288,256]{2,1,0:T(8,128)(2,1)S(1)}, u32[]{:S(2)}, u32[]{:S(2)}) collective-permute-start(bf16[4,288,256]{2,1,0:T(8,128)(2,1)} %get-tuple-element.33), channel_id=1, source_target_pairs={{0,16},{8,24},{16,0},{24,8},{1,17},{9,25},{17,1},{25,9},{2,18},{10... | collective-permute-start | bytes 1769480 | tf_op jit(solution)/shard_map/ppermute | solution.py:12
  73.5 18.1 %collective-permute-start.10 = (bf16[288,256]{1,0:T(8,128)(2,1)S(1)}, bf16[288,256]{1,0:T(8,128)(2,1)S(1)}, u32[]{:S(2)}, u32[]{:S(2)}) collective-permute-start(bf16[288,256]{1,0:T(8,128)(2,1)S(1)} %get-tuple-element.35), channel_id=1, source_target_pairs={{0,6},{1,7},{2,4},{3,5},{4,2},{5,3},{6,0},{7,1},{8,14},{9,15},{10,... | collective-permute-start | bytes 442376 | tf_op jit(solution)/shard_map/ppermute | solution.py:12
  76.5 17.9 %collective-permute-start.9 = (bf16[288,256]{1,0:T(8,128)(2,1)S(1)}, bf16[288,256]{1,0:T(8,128)(2,1)S(1)}, u32[]{:S(2)}, u32[]{:S(2)}) collective-permute-start(bf16[288,256]{1,0:T(8,128)(2,1)S(1)} %get-tuple-element.36), channel_id=1, source_target_pairs={{0,4},{1,5},{2,6},{3,7},{4,0},{5,1},{6,2},{7,3},{8,12},{9,13},{10,... | collective-permute-start | bytes 442376 | tf_op jit(solution)/shard_map/ppermute | solution.py:12
  86.6 8.0 %collective-permute-start.28 = (f32[2304]{0:T(1024)S(1)}, f32[2304]{0:T(1024)S(1)}, u32[]{:S(2)}, u32[]{:S(2)}) collective-permute-start(f32[2304]{0:T(1024)S(1)} %add_add_fusion.1), channel_id=1, source_target_pairs={{0,7},{1,6},{2,5},{3,4},{4,3},{5,2},{6,1},{7,0},{8,15},{9,14},{10,... | collective-permute-start | bytes 27656 | tf_op jit(solution)/shard_map/ppermute | solution.py:12
  90.5 9.1 %collective-permute-start.26 = (f32[2304]{0:T(1024)S(1)}, f32[2304]{0:T(1024)S(1)}, u32[]{:S(2)}, u32[]{:S(2)}) collective-permute-start(f32[2304]{0:T(1024)S(1)} %add_add_fusion.1), channel_id=1, source_target_pairs={{0,5},{1,4},{2,7},{3,6},{4,1},{5,0},{6,3},{7,2},{8,13},{9,12},{10,... | collective-permute-start | bytes 27656 | tf_op jit(solution)/shard_map/ppermute | solution.py:12
  91.6 8.2 %collective-permute-start.25 = (f32[2304]{0:T(1024)S(1)}, f32[2304]{0:T(1024)S(1)}, u32[]{:S(2)}, u32[]{:S(2)}) collective-permute-start(f32[2304]{0:T(1024)S(1)} %add_add_fusion.1), channel_id=1, source_target_pairs={{0,4},{1,5},{2,6},{3,7},{4,0},{5,1},{6,2},{7,3},{8,12},{9,13},{10,... | collective-permute-start | bytes 27656 | tf_op jit(solution)/shard_map/ppermute | solution.py:12
  94.7 9.3 %collective-permute-start.23 = (f32[2304]{0:T(1024)S(1)}, f32[2304]{0:T(1024)S(1)}, u32[]{:S(2)}, u32[]{:S(2)}) collective-permute-start(f32[2304]{0:T(1024)S(1)} %add_add_fusion.1), channel_id=1, source_target_pairs={{0,2},{1,3},{2,0},{3,1},{4,6},{5,7},{6,4},{7,5},{8,10},{9,11},{10,... | collective-permute-start | bytes 27656 | tf_op jit(solution)/shard_map/ppermute | solution.py:12
  96.3 8.8 %collective-permute-start.22 = (f32[2304]{0:T(1024)S(1)}, f32[2304]{0:T(1024)S(1)}, u32[]{:S(2)}, u32[]{:S(2)}) collective-permute-start(f32[2304]{0:T(1024)S(1)} %add_add_fusion.1), channel_id=1, source_target_pairs={{0,1},{1,0},{2,3},{3,2},{4,5},{5,4},{6,7},{7,6},{8,9},{9,8},{10,11... | collective-permute-start | bytes 27656 | tf_op jit(solution)/shard_map/ppermute | solution.py:12
  99.6 10.7 %collective-permute-start.8 = (bf16[288,256]{1,0:T(8,128)(2,1)S(1)}, bf16[288,256]{1,0:T(8,128)(2,1)S(1)}, u32[]{:S(2)}, u32[]{:S(2)}) collective-permute-start(bf16[288,256]{1,0:T(8,128)(2,1)S(1)} %get-tuple-element.37), channel_id=1, source_target_pairs={{0,2},{1,3},{2,0},{3,1},{4,6},{5,7},{6,4},{7,5},{8,10},{9,11},{10,... | collective-permute-start | bytes 442376 | tf_op jit(solution)/shard_map/ppermute | solution.py:12
  99.9 10.5 %collective-permute-start.6 = (bf16[288,256]{1,0:T(8,128)(2,1)S(1)}, bf16[288,256]{1,0:T(8,128)(2,1)S(1)}, u32[]{:S(2)}, u32[]{:S(2)}) collective-permute-start(bf16[288,256]{1,0:T(8,128)(2,1)S(1)} %get-tuple-element.38), channel_id=1, source_target_pairs={{0,7},{1,6},{2,5},{3,4},{4,3},{5,2},{6,1},{7,0},{8,15},{9,14},{10,... | collective-permute-start | bytes 442376 | tf_op jit(solution)/shard_map/ppermute | solution.py:12
  102.2 13.2 %collective-permute-start.5 = (bf16[288,256]{1,0:T(8,128)(2,1)S(1)}, bf16[288,256]{1,0:T(8,128)(2,1)S(1)}, u32[]{:S(2)}, u32[]{:S(2)}) collective-permute-start(bf16[288,256]{1,0:T(8,128)(2,1)S(1)} %get-tuple-element.39), channel_id=1, source_target_pairs={{0,5},{1,4},{2,7},{3,6},{4,1},{5,0},{6,3},{7,2},{8,13},{9,12},{10,... | collective-permute-start | bytes 442376 | tf_op jit(solution)/shard_map/ppermute | solution.py:12
  104.0 11.5 %collective-permute-start.4 = (bf16[288,256]{1,0:T(8,128)(2,1)S(1)}, bf16[288,256]{1,0:T(8,128)(2,1)S(1)}, u32[]{:S(2)}, u32[]{:S(2)}) collective-permute-start(bf16[288,256]{1,0:T(8,128)(2,1)S(1)} %get-tuple-element.40), channel_id=1, source_target_pairs={{0,3},{1,2},{2,1},{3,0},{4,7},{5,6},{6,5},{7,4},{8,11},{9,10},{10,... | collective-permute-start | bytes 442376 | tf_op jit(solution)/shard_map/ppermute | solution.py:12
  105.2 11.5 %collective-permute-start.3 = (bf16[288,256]{1,0:T(8,128)(2,1)S(1)}, bf16[288,256]{1,0:T(8,128)(2,1)S(1)}, u32[]{:S(2)}, u32[]{:S(2)}) collective-permute-start(bf16[288,256]{1,0:T(8,128)(2,1)S(1)} %get-tuple-element.41), channel_id=1, source_target_pairs={{0,1},{1,0},{2,3},{3,2},{4,5},{5,4},{6,7},{7,6},{8,9},{9,8},{10,11... | collective-permute-start | bytes 442376 | tf_op jit(solution)/shard_map/ppermute | solution.py:12
  (11 other events, 119.6 us)
